TPU v7x, 32 devices: a whole 2x2x4 slice. The times are simulated.
32 devices in a mesh: lat: 8 (over y, x, core), lon: 4 (over z).
Axes of the slice: x: 2, y: 2, z: 4, core: 2. Of those that a mesh axis runs over, the one named last changes fastest.
Arguments:
- inputs: bfloat16 [128, 384, 256], P('lat', 'lon'), may hold values from -6 to 6
- first_filter: bfloat16 [3, 3, 256, 256], replicated, may hold values from -0.125 to 0.125
- second_filter: bfloat16 [3, 3, 256, 256], replicated, may hold values from -0.125 to 0.125
- cotangent: bfloat16 [128, 384, 256], P('lat', 'lon'), may hold values from -30 to 30
Outputs:
- input_grad: bfloat16 [128, 384, 256], P('lat', 'lon')
- first_grad: float32 [3, 3, 256, 256], replicated
- second_grad: float32 [3, 3, 256, 256], replicated
All inputs are finite; a program needn't handle non-finite values.
Results may differ from a plain program's by a relative error of at most 0.0061.
Values may be sent and summed in bfloat16 or wider, within the bound.
A program may use at most 64 MiB of HBM per device.

v0:
```python
import jax
import jax.numpy as jnp
from jax import lax
from jax.sharding import PartitionSpec as P


def extended(block, sides, width):
    for axis, dim in sides:
        count = lax.axis_size(axis)
        forward = [(i, i + 1) for i in range(count - 1)]
        forward.append((count - 1, 0))
        backward = [(target, source) for source, target in forward]
        low = lax.ppermute(
            lax.slice_in_dim(block, block.shape[dim] - width, None, axis=dim), axis, forward
        )
        high = lax.ppermute(lax.slice_in_dim(block, 0, width, axis=dim), axis, backward)
        block = jnp.concatenate([low, block, high], axis=dim)
    return block


def mask_rows(padded, width):
    rows = padded.shape[0] - 2 * width
    position = lax.broadcasted_iota(jnp.int32, (padded.shape[0], 1, 1), 0)
    index = lax.axis_index("lat")
    count = lax.axis_size("lat")
    dropped = (position < width) & (index == 0) | (position >= rows + width) & (index == count - 1)
    return jnp.where(dropped, jnp.zeros((), padded.dtype), padded)


def extend(field):
    padded = extended(field, (("lat", 0), ("lon", 1)), 1)
    return mask_rows(padded, 1)


def conv_taps(padded, weight, rows, cols, flipped):
    total = jnp.zeros(
        (rows * cols, weight.shape[3] if not flipped else weight.shape[2]), jnp.float32
    )
    for first in range(3):
        for second in range(3):
            piece = padded[first : first + rows, second : second + cols, :].reshape(rows * cols, -1)
            if flipped:
                total = total + lax.dot_general(
                    piece,
                    weight[2 - first, 2 - second],
                    (((1,), (1,)), ((), ())),
                    preferred_element_type=jnp.float32,
                )
            else:
                total = total + jnp.dot(
                    piece, weight[first, second], preferred_element_type=jnp.float32
                )
    return total.reshape(rows, cols, -1)


def filter_grad(padded, delta, rows, cols):
    flat = delta.reshape(rows * cols, -1)
    taps = []
    for first in range(3):
        for second in range(3):
            piece = padded[first : first + rows, second : second + cols, :].reshape(rows * cols, -1)
            taps.append(
                lax.dot_general(
                    piece, flat, (((0,), (0,)), ((), ())), preferred_element_type=jnp.float32
                )
            )
    return jnp.stack(taps).reshape(3, 3, flat.shape[1], flat.shape[1])


def gelu_value(value):
    return value * 0.5 * (1.0 + jax.scipy.special.erf(value * 0.7071067811865476))


def gelu_slope(value):
    return (
        0.5 * (1.0 + jax.scipy.special.erf(value * 0.7071067811865476))
        + value * jnp.exp(-0.5 * value * value) * 0.3989422804014327
    )


def body(inputs, first_filter, second_filter, cotangent):
    rows, cols = (inputs.shape[0], inputs.shape[1])
    padded_in = extend(inputs)
    hidden_one = conv_taps(padded_in, first_filter, rows, cols, False)
    act = gelu_value(hidden_one).astype(jnp.bfloat16)
    padded_act = extend(act)
    hidden_two = conv_taps(padded_act, second_filter, rows, cols, False)
    delta_two = (cotangent.astype(jnp.float32) * gelu_slope(hidden_two)).astype(jnp.bfloat16)
    second_part = filter_grad(padded_act, delta_two, rows, cols)
    act_grad = conv_taps(extend(delta_two), second_filter, rows, cols, True)
    delta_one = (act_grad * gelu_slope(hidden_one)).astype(jnp.bfloat16)
    first_part = filter_grad(padded_in, delta_one, rows, cols)
    first_grad, second_grad = lax.psum((first_part, second_part), ("lat", "lon"))
    input_grad = conv_taps(extend(delta_one), first_filter, rows, cols, True).astype(jnp.bfloat16)
    return (input_grad, first_grad, second_grad)


def solution(mesh):
    in_specs = (P("lat", "lon", None), P(), P(), P("lat", "lon", None))
    out_specs = (P("lat", "lon", None), P(), P())
    return jax.shard_map(body, mesh=mesh, in_specs=in_specs, out_specs=out_specs, check_vma=False)
```

profile of v0, /device:TPU:0, one launch (start us, length us, event | category | flops | bytes accessed | tf_op | source)
XLA Modules:
  0.0 228.8 jit_solution(7460417335077282387)
XLA Ops:
  7.2 0.8 fusion.133
  8.0 0.5 collective-permute-start
  8.6 2.9 %collective-permute-start.1 = (bf16[1,96,256]{2,1,0:T(8,128)(2,1)S(1)}, bf16[1,96,256]{2,1,0:T(8,128)(2,1)S(1)}, u32[]{:S(2)}, u32[]{:S(2)}) collective-permute-start(bf16[1,96,256]{2,1,0:T(8,128)(2,1)S(1)} %get-tuple-element.55), channel_id=1, source_target_pairs={{4,0},{8,4},{12,8},{16,12},{20,16},{24,20},{28,24},{0,28},{5,1},{9... | collective-permute-start | bytes 147464 | tf_op jit(solution)/shard_map/ppermute | solution.py:16
  11.5 1.7 collective-permute-done
  13.2 1.2 constant_dynamic-update-slice_fusion.1
  14.5 4.4 %collective-permute-start.3 = (bf16[18,1,256]{2,1,0:T(2,128)(2,1)S(1)}, bf16[18,1,256]{2,1,0:T(2,128)(2,1)S(1)}, u32[]{:S(2)}, u32[]{:S(2)}) collective-permute-start(bf16[18,1,256]{2,1,0:T(2,128)(2,1)S(1)} %get-tuple-element.48), channel_id=1, source_target_pairs={{1,0},{2,1},{3,2},{0,3},{5,4},{6,5},{7,6},{4,7},{9,8},{10,9},{11,1... | collective-permute-start | bytes 27656 | tf_op jit(solution)/shard_map/ppermute | solution.py:16
  18.9 1.5 collective-permute-done.3
  20.3 4.1 %collective-permute-done.2 = bf16[18,1,256]{2,1,0:T(2,128)(2,1)S(1)} collective-permute-done((bf16[18,1,256]{2,1,0:T(2,128)(2,1)S(1)}, bf16[18,1,256]{2,1,0:T(2,128)(2,1)S(1)}, u32[]{:S(2)}, u32[]{:S(2)}) %collective-permute-start.2) | collective-permute-done | bytes 9248 | tf_op jit(solution)/shard_map/ppermute | solution.py:13
  24.4 0.6 maximum_select_fusion
  25.0 0.8 fusion.128
  25.9 0.4 copy-done.1
  30.0 0.5 collective-permute-start.4
  30.5 1.4 collective-permute-done.5
  31.9 2.6 %collective-permute-done.4 = bf16[1,96,256]{2,1,0:T(8,128)(2,1)S(1)} collective-permute-done((bf16[1,96,256]{2,1,0:T(8,128)(2,1)S(1)}, bf16[1,96,256]{2,1,0:T(8,128)(2,1)S(1)}, u32[]{:S(2)}, u32[]{:S(2)}) %collective-permute-start.4) | collective-permute-done | bytes 49184 | tf_op jit(solution)/shard_map/ppermute | solution.py:13
  34.8 1.8 collective-permute-start.6
  36.6 1.7 collective-permute-done.7
  38.4 2.0 collective-permute-done.6
  40.4 0.6 maximum_select_fusion.1
  40.9 1.1 fusion.127
  45.5 0.7 copy-done.5
  46.3 0.7 fusion.6
  47.0 0.4 fusion.21
  47.5 0.5 collective-permute-start.8
  48.0 0.4 fusion.20
  48.4 0.4 fusion.19
  48.8 0.4 fusion.18
  49.3 0.4 fusion.17
  49.7 0.4 fusion.16
  50.1 0.4 fusion.15
  50.5 0.4 fusion.14
  51.0 1.1 collective-permute-done.8
  52.2 2.0 collective-permute-start.10
  54.2 0.4 fusion.13
  54.7 1.3 collective-permute-done.11
  56.0 1.9 collective-permute-done.10
  57.8 0.6 maximum_select_fusion.2
  58.4 1.1 fusion.126
  63.1 0.7 fusion.12
  64.2 0.6 collective-permute-start.13
  64.8 0.4 fusion.29
  65.2 0.4 fusion.28
  65.7 0.4 fusion.27
  66.1 0.4 fusion.26
  66.5 0.4 fusion.25
  66.9 0.4 fusion.24
  67.4 0.4 fusion.23
  67.8 1.4 collective-permute-done.12
  69.3 2.0 collective-permute-start.14
  71.3 0.4 fusion.22
  71.8 1.4 copy-done.4
  73.2 2.0 collective-permute-done.14
  75.1 0.6 maximum_select_fusion.3
  75.7 1.1 fusion.125
  77.2 0.4 convolution_add_fusion.7
  77.6 0.4 convolution_add_fusion.6
  78.0 0.4 convolution_add_fusion.5
  78.4 0.4 convolution_add_fusion.4
  78.9 0.4 convolution_add_fusion.3
  79.3 0.4 convolution_add_fusion.2
  79.7 0.4 convolution_add_fusion.1
  80.1 1.3 fusion
  81.4 135.8 %all-reduce.3.cloned.1.call-done = (f32[3,3,256,256]{3,2,1,0:T(8,128)}, f32[3,3,256,256]{3,2,1,0:T(8,128)}) async-done(((f32[3,3,256,256]{3,2,1,0:T(8,128)}, f32[3,3,256,256]{3,2,1,0:T(8,128)}), (f32[3,3,256,256]{3,2,1,0:T(8,128)}, f32[3,3,256,256]{3,2,1,0:T(8,128)})) %all-reduce.3.cloned.1.call-update) | async-done | bytes 4718608 | tf_op jit(solution)/shard_map/psum | solution.py:93
  217.2 3.4 %copy.27 = f32[3,3,256,256]{3,2,1,0:T(8,128)} copy(f32[3,3,256,256]{3,2,1,0:T(8,128)} %get-tuple-element.58) | data formatting | bytes 4718592
  220.5 1.4 copy.28
  (62 shorter events, 12.2 us)
Async XLA Ops:
  7.2 210.0 %all-reduce.3.cloned.1.call-start = ((), (), s32[]{:S(2)}) async-start(), calls=%async_computation | async-start | bytes 9437184 | tf_op jit(solution)/shard_map/psum | solution.py:93
  8.0 5.2 %collective-permute-start = (bf16[1,96,256]{2,1,0:T(8,128)(2,1)S(1)}, bf16[1,96,256]{2,1,0:T(8,128)(2,1)S(1)}, u32[]{:S(2)}, u32[]{:S(2)}) collective-permute-start(bf16[1,96,256]{2,1,0:T(8,128)(2,1)S(1)} %get-tuple-element.56), channel_id=1, source_target_pairs={{0,4},{4,8},{8,12},{12,16},{16,20},{20,24},{24,28},{28,0},{1,5},{5... | collective-permute-start | bytes 147464 | tf_op jit(solution)/shard_map/ppermute | solution.py:13
  8.6 5.8 %collective-permute-start.1 = (bf16[1,96,256]{2,1,0:T(8,128)(2,1)S(1)}, bf16[1,96,256]{2,1,0:T(8,128)(2,1)S(1)}, u32[]{:S(2)}, u32[]{:S(2)}) collective-permute-start(bf16[1,96,256]{2,1,0:T(8,128)(2,1)S(1)} %get-tuple-element.55), channel_id=1, source_target_pairs={{4,0},{8,4},{12,8},{16,12},{20,16},{24,20},{28,24},{0,28},{5,1},{9... | collective-permute-start | bytes 147464 | tf_op jit(solution)/shard_map/ppermute | solution.py:16
  14.5 5.9 %collective-permute-start.3 = (bf16[18,1,256]{2,1,0:T(2,128)(2,1)S(1)}, bf16[18,1,256]{2,1,0:T(2,128)(2,1)S(1)}, u32[]{:S(2)}, u32[]{:S(2)}) collective-permute-start(bf16[18,1,256]{2,1,0:T(2,128)(2,1)S(1)} %get-tuple-element.48), channel_id=1, source_target_pairs={{1,0},{2,1},{3,2},{0,3},{5,4},{6,5},{7,6},{4,7},{9,8},{10,9},{11,1... | collective-permute-start | bytes 27656 | tf_op jit(solution)/shard_map/ppermute | solution.py:16
  18.9 5.6 %collective-permute-start.2 = (bf16[18,1,256]{2,1,0:T(2,128)(2,1)S(1)}, bf16[18,1,256]{2,1,0:T(2,128)(2,1)S(1)}, u32[]{:S(2)}, u32[]{:S(2)}) collective-permute-start(bf16[18,1,256]{2,1,0:T(2,128)(2,1)S(1)} %get-tuple-element.47), channel_id=1, source_target_pairs={{0,1},{1,2},{2,3},{3,0},{4,5},{5,6},{6,7},{7,4},{8,9},{9,10},{10,1... | collective-permute-start | bytes 27656 | tf_op jit(solution)/shard_map/ppermute | solution.py:13
  25.0 1.3 copy-start.1
  30.0 2.0 collective-permute-start.5
  30.0 4.5 %collective-permute-start.4 = (bf16[1,96,256]{2,1,0:T(8,128)(2,1)S(1)}, bf16[1,96,256]{2,1,0:T(8,128)(2,1)S(1)}, u32[]{:S(2)}, u32[]{:S(2)}) collective-permute-start(bf16[1,96,256]{2,1,0:T(8,128)(2,1)S(1)} %get-tuple-element.53), channel_id=1, source_target_pairs={{0,4},{4,8},{8,12},{12,16},{16,20},{20,24},{24,28},{28,0},{1,5},{5... | collective-permute-start | bytes 147464 | tf_op jit(solution)/shard_map/ppermute | solution.py:13
  34.5 3.8 %collective-permute-start.7 = (bf16[18,1,256]{2,1,0:T(2,128)(2,1)S(1)}, bf16[18,1,256]{2,1,0:T(2,128)(2,1)S(1)}, u32[]{:S(2)}, u32[]{:S(2)}) collective-permute-start(bf16[18,1,256]{2,1,0:T(2,128)(2,1)S(1)} %get-tuple-element.46), channel_id=1, source_target_pairs={{1,0},{2,1},{3,2},{0,3},{5,4},{6,5},{7,6},{4,7},{9,8},{10,9},{11,1... | collective-permute-start | bytes 27656 | tf_op jit(solution)/shard_map/ppermute | solution.py:16
  34.8 5.6 %collective-permute-start.6 = (bf16[18,1,256]{2,1,0:T(2,128)(2,1)S(1)}, bf16[18,1,256]{2,1,0:T(2,128)(2,1)S(1)}, u32[]{:S(2)}, u32[]{:S(2)}) collective-permute-start(bf16[18,1,256]{2,1,0:T(2,128)(2,1)S(1)} %get-tuple-element.45), channel_id=1, source_target_pairs={{0,1},{1,2},{2,3},{3,0},{4,5},{5,6},{6,7},{7,4},{8,9},{9,10},{10,1... | collective-permute-start | bytes 27656 | tf_op jit(solution)/shard_map/ppermute | solution.py:13
  40.9 1.3 copy-start
  45.1 1.1 copy-start.5
  47.4 3.6 %collective-permute-start.9 = (bf16[1,96,256]{2,1,0:T(8,128)(2,1)S(1)}, bf16[1,96,256]{2,1,0:T(8,128)(2,1)S(1)}, u32[]{:S(2)}, u32[]{:S(2)}) collective-permute-start(bf16[1,96,256]{2,1,0:T(8,128)(2,1)S(1)} %get-tuple-element.52), channel_id=1, source_target_pairs={{4,0},{8,4},{12,8},{16,12},{20,16},{24,20},{28,24},{0,28},{5,1},{9... | collective-permute-start | bytes 147464 | tf_op jit(solution)/shard_map/ppermute | solution.py:16
  47.5 4.6 %collective-permute-start.8 = (bf16[1,96,256]{2,1,0:T(8,128)(2,1)S(1)}, bf16[1,96,256]{2,1,0:T(8,128)(2,1)S(1)}, u32[]{:S(2)}, u32[]{:S(2)}) collective-permute-start(bf16[1,96,256]{2,1,0:T(8,128)(2,1)S(1)} %get-tuple-element.51), channel_id=1, source_target_pairs={{0,4},{4,8},{8,12},{12,16},{16,20},{20,24},{24,28},{28,0},{1,5},{5... | collective-permute-start | bytes 147464 | tf_op jit(solution)/shard_map/ppermute | solution.py:13
  52.2 3.8 %collective-permute-start.11 = (bf16[18,1,256]{2,1,0:T(2,128)(2,1)S(1)}, bf16[18,1,256]{2,1,0:T(2,128)(2,1)S(1)}, u32[]{:S(2)}, u32[]{:S(2)}) collective-permute-start(bf16[18,1,256]{2,1,0:T(2,128)(2,1)S(1)} %get-tuple-element.44), channel_id=1, source_target_pairs={{1,0},{2,1},{3,2},{0,3},{5,4},{6,5},{7,6},{4,7},{9,8},{10,9},{11,1... | collective-permute-start | bytes 27656 | tf_op jit(solution)/shard_map/ppermute | solution.py:16
  52.2 5.6 %collective-permute-start.10 = (bf16[18,1,256]{2,1,0:T(2,128)(2,1)S(1)}, bf16[18,1,256]{2,1,0:T(2,128)(2,1)S(1)}, u32[]{:S(2)}, u32[]{:S(2)}) collective-permute-start(bf16[18,1,256]{2,1,0:T(2,128)(2,1)S(1)} %get-tuple-element.43), channel_id=1, source_target_pairs={{0,1},{1,2},{2,3},{3,0},{4,5},{5,6},{6,7},{7,4},{8,9},{9,10},{10,1... | collective-permute-start | bytes 27656 | tf_op jit(solution)/shard_map/ppermute | solution.py:13
  54.7 4.8 %copy-start.3 = (f32[9,256,256]{2,1,0:T(8,128)}, f32[9,256,256]{2,1,0:T(8,128)S(1)}, u32[]{:S(2)}) copy-start(f32[9,256,256]{2,1,0:T(8,128)S(1)} %fusion.13) | copy-start | bytes 7077892
  64.2 3.6 %collective-permute-start.13 = (bf16[1,96,256]{2,1,0:T(8,128)(2,1)S(1)}, bf16[1,96,256]{2,1,0:T(8,128)(2,1)S(1)}, u32[]{:S(2)}, u32[]{:S(2)}) collective-permute-start(bf16[1,96,256]{2,1,0:T(8,128)(2,1)S(1)} %get-tuple-element.50), channel_id=1, source_target_pairs={{4,0},{8,4},{12,8},{16,12},{20,16},{24,20},{28,24},{0,28},{5,1},{9... | collective-permute-start | bytes 147464 | tf_op jit(solution)/shard_map/ppermute | solution.py:16
  64.8 4.4 %collective-permute-start.12 = (bf16[1,96,256]{2,1,0:T(8,128)(2,1)S(1)}, bf16[1,96,256]{2,1,0:T(8,128)(2,1)S(1)}, u32[]{:S(2)}, u32[]{:S(2)}) collective-permute-start(bf16[1,96,256]{2,1,0:T(8,128)(2,1)S(1)} %get-tuple-element.49), channel_id=1, source_target_pairs={{0,4},{4,8},{8,12},{12,16},{16,20},{20,24},{24,28},{28,0},{1,5},{5... | collective-permute-start | bytes 147464 | tf_op jit(solution)/shard_map/ppermute | solution.py:13
  69.2 3.9 %collective-permute-start.15 = (bf16[18,1,256]{2,1,0:T(2,128)(2,1)S(1)}, bf16[18,1,256]{2,1,0:T(2,128)(2,1)S(1)}, u32[]{:S(2)}, u32[]{:S(2)}) collective-permute-start(bf16[18,1,256]{2,1,0:T(2,128)(2,1)S(1)} %get-tuple-element.42), channel_id=1, source_target_pairs={{1,0},{2,1},{3,2},{0,3},{5,4},{6,5},{7,6},{4,7},{9,8},{10,9},{11,1... | collective-permute-start | bytes 27656 | tf_op jit(solution)/shard_map/ppermute | solution.py:16
  69.3 5.8 %collective-permute-start.14 = (bf16[18,1,256]{2,1,0:T(2,128)(2,1)S(1)}, bf16[18,1,256]{2,1,0:T(2,128)(2,1)S(1)}, u32[]{:S(2)}, u32[]{:S(2)}) collective-permute-start(bf16[18,1,256]{2,1,0:T(2,128)(2,1)S(1)} %get-tuple-element.41), channel_id=1, source_target_pairs={{0,1},{1,2},{2,3},{3,0},{4,5},{5,6},{6,7},{7,4},{8,9},{9,10},{10,1... | collective-permute-start | bytes 27656 | tf_op jit(solution)/shard_map/ppermute | solution.py:13
  71.7 1.4 copy-start.4
  217.2 3.4 %copy-start.2 = (f32[3,3,256,256]{3,2,1,0:T(8,128)S(1)}, f32[3,3,256,256]{3,2,1,0:T(8,128)}, u32[]{:S(2)}) copy-start(f32[3,3,256,256]{3,2,1,0:T(8,128)} %get-tuple-element.59) | copy-start | bytes 7077892
Sparse Core Ops, SparseCore 0:
  73.3 143.8 all-reduce.2
where the time goes:
time: 229 us
  waiting for transfers between devices  158 us (69%)
  matrix products  22.3 us (10%)
  starting transfers between devices  15.8 us (7%)
  between operations  14.6 us (6%)
  local copies, waits for them, and re-layouts  13.6 us (6%)
  other arithmetic  4.03 us (2%)
    psum x1, waiting for transfers between devices, body(): lax.psum((first_part, second_part), ('lat', 'lon'))  136 us
    ppermute x8, waiting for transfers between devices, extended(): lax.ppermute(lax.slice_in_dim(block, block.shape[dim] - width, None, axis...  16.7 us
    unnamed x16, local copies, waits for them, and re-layouts  8.77 us
    ppermute x8, starting transfers between devices, extended(): lax.ppermute(lax.slice_in_dim(block, 0, width, axis=dim), axis, backward)  8.4 us
    dot_general x18, matrix products, conv_taps(): lax.dot_general(piece, weight[2 - first, 2 - second], (((1,), (1,)), ((),...  8.18 us
    dot_general x18, matrix products, filter_grad(): lax.dot_general(piece, flat, (((0,), (0,)), ((), ())), preferred_element_...  7.54 us
    ppermute x8, starting transfers between devices, extended(): lax.ppermute(lax.slice_in_dim(block, block.shape[dim] - width, None, axis...  7.38 us
    dot_general x18, matrix products, conv_taps(): jnp.dot(piece, weight[first, second], preferred_element_type=jnp.float32)  6.59 us
  transfers between devices with their start and end apart: 17, of which 13 were waited for; matrix products, arithmetic and copies ran while one was open for 6% of the time, Pallas kernels for 0%

commit v1 on v0

--- a/solution.py
+++ b/solution.py
@@ -90,7 +90,7 @@
     act_grad = conv_taps(extend(delta_two), second_filter, rows, cols, True)
     delta_one = (act_grad * gelu_slope(hidden_one)).astype(jnp.bfloat16)
     first_part = filter_grad(padded_in, delta_one, rows, cols)
-    first_grad, second_grad = lax.psum((first_part, second_part), ("lat", "lon"))
+    first_grad, second_grad = lax.psum(lax.psum((first_part, second_part), "lat"), "lon")
     input_grad = conv_taps(extend(delta_one), first_filter, rows, cols, True).astype(jnp.bfloat16)
     return (input_grad, first_grad, second_grad)
 

time: 229 us -> 340 us (1.48)
  waiting for transfers between devices: 158 us -> 267 us
    psum x1 -> x2, waiting for transfers between devices: 136 us -> 238 us  [the longest x1 153 us: body(): lax.psum(lax.psum((first_part, second_part), 'lat'), 'lon')]
    ppermute x8, waiting for transfers between devices: 5.89 us -> 9.75 us  [extended(): lax.ppermute(lax.slice_in_dim(block, 0, width, axis=dim), axis, backward)]
    ppermute x8, starting transfers between devices: 8.4 us -> 12.1 us  [extended(): lax.ppermute(lax.slice_in_dim(block, 0, width, axis=dim), axis, backward)]
  transfers between devices with their start and end apart: 17 -> 18, of which waited for: 13 -> 16; matrix products, arithmetic and copies ran while one was open for 6% -> 3% of each run, Pallas kernels for 0% -> 0%
where the time goes in v1:
time: 340 us
  waiting for transfers between devices  267 us (79%)
  matrix products  22.3 us (7%)
  starting transfers between devices  17.6 us (5%)
  between operations  14.6 us (4%)
  local copies, waits for them, and re-layouts  13.6 us (4%)
  other arithmetic  4.03 us (1%)
    psum x1, waiting for transfers between devices, body(): lax.psum(lax.psum((first_part, second_part), 'lat'), 'lon')  153 us
    psum x1, waiting for transfers between devices, body(): lax.psum((first_part, second_part), 'lat')  84.2 us
    ppermute x8, waiting for transfers between devices, extended(): lax.ppermute(lax.slice_in_dim(block, block.shape[dim] - width, None, axis...  20 us
    ppermute x8, starting transfers between devices, extended(): lax.ppermute(lax.slice_in_dim(block, 0, width, axis=dim), axis, backward)  12.1 us
    ppermute x8, waiting for transfers between devices, extended(): lax.ppermute(lax.slice_in_dim(block, 0, width, axis=dim), axis, backward)  9.75 us
    unnamed x16, local copies, waits for them, and re-layouts  8.77 us
    dot_general x18, matrix products, conv_taps(): lax.dot_general(piece, weight[2 - first, 2 - second], (((1,), (1,)), ((),...  8.18 us
    dot_general x18, matrix products, filter_grad(): lax.dot_general(piece, flat, (((0,), (0,)), ((), ())), preferred_element_...  7.53 us
  transfers between devices with their start and end apart: 18, of which 16 were waited for; matrix products, arithmetic and copies ran while one was open for 3% of the time, Pallas kernels for 0%

profile of v1, /device:TPU:0, one launch (start us, length us, event | category | flops | bytes accessed | tf_op | source)
XLA Modules:
  0.0 339.5 jit_solution(3851944277064034261)
XLA Ops:
  7.2 0.8 fusion.133
  8.0 0.5 collective-permute-start
  8.6 2.9 collective-permute-start.1
  11.5 1.7 collective-permute-done
  13.2 1.2 constant_dynamic-update-slice_fusion.1
  14.5 4.4 %collective-permute-start.3 = (bf16[18,1,256]{2,1,0:T(2,128)(2,1)S(1)}, bf16[18,1,256]{2,1,0:T(2,128)(2,1)S(1)}, u32[]{:S(2)}, u32[]{:S(2)}) collective-permute-start(bf16[18,1,256]{2,1,0:T(2,128)(2,1)S(1)} %get-tuple-element.50), channel_id=1, source_target_pairs={{1,0},{2,1},{3,2},{0,3},{5,4},{6,5},{7,6},{4,7},{9,8},{10,9},{11,1... | collective-permute-start | bytes 27656 | tf_op jit(solution)/shard_map/ppermute | solution.py:16
  18.9 1.5 collective-permute-done.3
  20.3 4.1 %collective-permute-done.2 = bf16[18,1,256]{2,1,0:T(2,128)(2,1)S(1)} collective-permute-done((bf16[18,1,256]{2,1,0:T(2,128)(2,1)S(1)}, bf16[18,1,256]{2,1,0:T(2,128)(2,1)S(1)}, u32[]{:S(2)}, u32[]{:S(2)}) %collective-permute-start.2) | collective-permute-done | bytes 9248 | tf_op jit(solution)/shard_map/ppermute | solution.py:13
  24.4 0.6 maximum_select_fusion
  25.0 0.8 fusion.128
  25.9 0.4 copy-done.1
  30.0 0.5 collective-permute-start.4
  30.5 1.4 collective-permute-done.5
  31.9 2.6 collective-permute-done.4
  34.8 1.8 collective-permute-start.6
  36.6 1.7 collective-permute-done.7
  38.4 2.0 collective-permute-done.6
  40.4 0.6 maximum_select_fusion.1
  40.9 1.1 fusion.127
  45.5 0.7 copy-done.5
  46.3 0.7 fusion.6
  47.5 0.5 collective-permute-start.8
  48.0 0.4 fusion.20
  48.4 0.4 fusion.19
  48.8 0.4 fusion.18
  49.3 0.4 fusion.17
  49.7 0.4 fusion.16
  50.1 0.4 fusion.15
  50.5 0.4 fusion.14
  51.0 1.1 collective-permute-done.8
  52.2 2.0 collective-permute-start.10
  54.2 0.4 fusion.13
  54.7 1.3 collective-permute-done.11
  56.0 1.9 collective-permute-done.10
  57.8 0.6 maximum_select_fusion.2
  58.4 1.1 fusion.126
  63.1 0.7 fusion.12
  64.2 0.4 fusion.29
  64.6 0.4 fusion.28
  65.5 0.4 fusion.26
  65.9 0.4 fusion.25
  66.3 0.4 fusion.24
  66.7 0.4 fusion.23
  67.2 0.4 fusion.22
  67.6 1.4 copy-done.4
  69.1 84.2 %all-reduce.5.cloned.1.call-done = (f32[3,3,256,256]{3,2,1,0:T(8,128)}, f32[3,3,256,256]{3,2,1,0:T(8,128)}) async-done(((f32[3,3,256,256]{3,2,1,0:T(8,128)}, f32[3,3,256,256]{3,2,1,0:T(8,128)}), (f32[3,3,256,256]{3,2,1,0:T(8,128)}, f32[3,3,256,256]{3,2,1,0:T(8,128)})) %all-reduce.5.cloned.1.call-update) | async-done | bytes 4718608 | tf_op jit(solution)/shard_map/psum | solution.py:93
  153.3 1.0 collective-permute-start.13
  154.3 2.1 collective-permute-done.13
  156.4 2.3 collective-permute-done.12
  158.7 3.4 collective-permute-start.15
  162.1 1.8 collective-permute-done.15
  163.9 4.3 %collective-permute-done.14 = bf16[18,1,256]{2,1,0:T(2,128)(2,1)S(1)} collective-permute-done((bf16[18,1,256]{2,1,0:T(2,128)(2,1)S(1)}, bf16[18,1,256]{2,1,0:T(2,128)(2,1)S(1)}, u32[]{:S(2)}, u32[]{:S(2)}) %collective-permute-start.14) | collective-permute-done | bytes 9248 | tf_op jit(solution)/shard_map/ppermute | solution.py:13
  168.2 0.6 maximum_select_fusion.3
  168.8 1.1 fusion.125
  170.3 0.4 convolution_add_fusion.7
  170.7 0.4 convolution_add_fusion.6
  171.1 0.4 convolution_add_fusion.5
  171.5 0.4 convolution_add_fusion.4
  171.9 0.4 convolution_add_fusion.3
  172.4 0.4 convolution_add_fusion.2
  173.2 1.3 fusion
  174.5 153.4 %all-reduce.7.cloned.1.call-done = (f32[3,3,256,256]{3,2,1,0:T(8,128)}, f32[3,3,256,256]{3,2,1,0:T(8,128)}) async-done(((f32[3,3,256,256]{3,2,1,0:T(8,128)}, f32[3,3,256,256]{3,2,1,0:T(8,128)}), (f32[3,3,256,256]{3,2,1,0:T(8,128)}, f32[3,3,256,256]{3,2,1,0:T(8,128)})) %all-reduce.7.cloned.1.call-update) | async-done | bytes 4718608 | tf_op jit(solution)/shard_map/psum | solution.py:93
  327.9 3.4 copy.29
  331.3 1.4 copy.30
  (65 shorter events, 13.4 us)
Async XLA Ops:
  7.2 146.1 %all-reduce.5.cloned.1.call-start = ((), (), s32[]{:S(2)}) async-start(), calls=%async_computation | async-start | bytes 9437184 | tf_op jit(solution)/shard_map/psum | solution.py:93
  8.0 5.2 %collective-permute-start = (bf16[1,96,256]{2,1,0:T(8,128)(2,1)S(1)}, bf16[1,96,256]{2,1,0:T(8,128)(2,1)S(1)}, u32[]{:S(2)}, u32[]{:S(2)}) collective-permute-start(bf16[1,96,256]{2,1,0:T(8,128)(2,1)S(1)} %get-tuple-element.58), channel_id=1, source_target_pairs={{0,4},{4,8},{8,12},{12,16},{16,20},{20,24},{24,28},{28,0},{1,5},{5... | collective-permute-start | bytes 147464 | tf_op jit(solution)/shard_map/ppermute | solution.py:13
  8.6 5.8 %collective-permute-start.1 = (bf16[1,96,256]{2,1,0:T(8,128)(2,1)S(1)}, bf16[1,96,256]{2,1,0:T(8,128)(2,1)S(1)}, u32[]{:S(2)}, u32[]{:S(2)}) collective-permute-start(bf16[1,96,256]{2,1,0:T(8,128)(2,1)S(1)} %get-tuple-element.57), channel_id=1, source_target_pairs={{4,0},{8,4},{12,8},{16,12},{20,16},{24,20},{28,24},{0,28},{5,1},{9... | collective-permute-start | bytes 147464 | tf_op jit(solution)/shard_map/ppermute | solution.py:16
  14.5 5.9 %collective-permute-start.3 = (bf16[18,1,256]{2,1,0:T(2,128)(2,1)S(1)}, bf16[18,1,256]{2,1,0:T(2,128)(2,1)S(1)}, u32[]{:S(2)}, u32[]{:S(2)}) collective-permute-start(bf16[18,1,256]{2,1,0:T(2,128)(2,1)S(1)} %get-tuple-element.50), channel_id=1, source_target_pairs={{1,0},{2,1},{3,2},{0,3},{5,4},{6,5},{7,6},{4,7},{9,8},{10,9},{11,1... | collective-permute-start | bytes 27656 | tf_op jit(solution)/shard_map/ppermute | solution.py:16
  18.9 5.6 %collective-permute-start.2 = (bf16[18,1,256]{2,1,0:T(2,128)(2,1)S(1)}, bf16[18,1,256]{2,1,0:T(2,128)(2,1)S(1)}, u32[]{:S(2)}, u32[]{:S(2)}) collective-permute-start(bf16[18,1,256]{2,1,0:T(2,128)(2,1)S(1)} %get-tuple-element.49), channel_id=1, source_target_pairs={{0,1},{1,2},{2,3},{3,0},{4,5},{5,6},{6,7},{7,4},{8,9},{9,10},{10,1... | collective-permute-start | bytes 27656 | tf_op jit(solution)/shard_map/ppermute | solution.py:13
  25.0 1.3 copy-start.1
  30.0 2.0 collective-permute-start.5
  30.0 4.5 %collective-permute-start.4 = (bf16[1,96,256]{2,1,0:T(8,128)(2,1)S(1)}, bf16[1,96,256]{2,1,0:T(8,128)(2,1)S(1)}, u32[]{:S(2)}, u32[]{:S(2)}) collective-permute-start(bf16[1,96,256]{2,1,0:T(8,128)(2,1)S(1)} %get-tuple-element.55), channel_id=1, source_target_pairs={{0,4},{4,8},{8,12},{12,16},{16,20},{20,24},{24,28},{28,0},{1,5},{5... | collective-permute-start | bytes 147464 | tf_op jit(solution)/shard_map/ppermute | solution.py:13
  34.5 3.8 %collective-permute-start.7 = (bf16[18,1,256]{2,1,0:T(2,128)(2,1)S(1)}, bf16[18,1,256]{2,1,0:T(2,128)(2,1)S(1)}, u32[]{:S(2)}, u32[]{:S(2)}) collective-permute-start(bf16[18,1,256]{2,1,0:T(2,128)(2,1)S(1)} %get-tuple-element.48), channel_id=1, source_target_pairs={{1,0},{2,1},{3,2},{0,3},{5,4},{6,5},{7,6},{4,7},{9,8},{10,9},{11,1... | collective-permute-start | bytes 27656 | tf_op jit(solution)/shard_map/ppermute | solution.py:16
  34.8 5.6 %collective-permute-start.6 = (bf16[18,1,256]{2,1,0:T(2,128)(2,1)S(1)}, bf16[18,1,256]{2,1,0:T(2,128)(2,1)S(1)}, u32[]{:S(2)}, u32[]{:S(2)}) collective-permute-start(bf16[18,1,256]{2,1,0:T(2,128)(2,1)S(1)} %get-tuple-element.47), channel_id=1, source_target_pairs={{0,1},{1,2},{2,3},{3,0},{4,5},{5,6},{6,7},{7,4},{8,9},{9,10},{10,1... | collective-permute-start | bytes 27656 | tf_op jit(solution)/shard_map/ppermute | solution.py:13
  40.9 1.3 copy-start
  45.1 1.1 copy-start.5
  47.4 3.6 %collective-permute-start.9 = (bf16[1,96,256]{2,1,0:T(8,128)(2,1)S(1)}, bf16[1,96,256]{2,1,0:T(8,128)(2,1)S(1)}, u32[]{:S(2)}, u32[]{:S(2)}) collective-permute-start(bf16[1,96,256]{2,1,0:T(8,128)(2,1)S(1)} %get-tuple-element.54), channel_id=1, source_target_pairs={{4,0},{8,4},{12,8},{16,12},{20,16},{24,20},{28,24},{0,28},{5,1},{9... | collective-permute-start | bytes 147464 | tf_op jit(solution)/shard_map/ppermute | solution.py:16
  47.5 4.6 %collective-permute-start.8 = (bf16[1,96,256]{2,1,0:T(8,128)(2,1)S(1)}, bf16[1,96,256]{2,1,0:T(8,128)(2,1)S(1)}, u32[]{:S(2)}, u32[]{:S(2)}) collective-permute-start(bf16[1,96,256]{2,1,0:T(8,128)(2,1)S(1)} %get-tuple-element.53), channel_id=1, source_target_pairs={{0,4},{4,8},{8,12},{12,16},{16,20},{20,24},{24,28},{28,0},{1,5},{5... | collective-permute-start | bytes 147464 | tf_op jit(solution)/shard_map/ppermute | solution.py:13
  52.2 3.8 %collective-permute-start.11 = (bf16[18,1,256]{2,1,0:T(2,128)(2,1)S(1)}, bf16[18,1,256]{2,1,0:T(2,128)(2,1)S(1)}, u32[]{:S(2)}, u32[]{:S(2)}) collective-permute-start(bf16[18,1,256]{2,1,0:T(2,128)(2,1)S(1)} %get-tuple-element.46), channel_id=1, source_target_pairs={{1,0},{2,1},{3,2},{0,3},{5,4},{6,5},{7,6},{4,7},{9,8},{10,9},{11,1... | collective-permute-start | bytes 27656 | tf_op jit(solution)/shard_map/ppermute | solution.py:16
  52.2 5.6 %collective-permute-start.10 = (bf16[18,1,256]{2,1,0:T(2,128)(2,1)S(1)}, bf16[18,1,256]{2,1,0:T(2,128)(2,1)S(1)}, u32[]{:S(2)}, u32[]{:S(2)}) collective-permute-start(bf16[18,1,256]{2,1,0:T(2,128)(2,1)S(1)} %get-tuple-element.45), channel_id=1, source_target_pairs={{0,1},{1,2},{2,3},{3,0},{4,5},{5,6},{6,7},{7,4},{8,9},{9,10},{10,1... | collective-permute-start | bytes 27656 | tf_op jit(solution)/shard_map/ppermute | solution.py:13
  54.7 4.8 %copy-start.3 = (f32[9,256,256]{2,1,0:T(8,128)}, f32[9,256,256]{2,1,0:T(8,128)S(1)}, u32[]{:S(2)}) copy-start(f32[9,256,256]{2,1,0:T(8,128)S(1)} %fusion.13) | copy-start | bytes 7077892
  67.6 1.4 copy-start.4
  69.0 258.9 %all-reduce.7.cloned.1.call-start = ((), (), s32[]{:S(2)}) async-start(), calls=%async_computation.1 | async-start | bytes 9437184 | tf_op jit(solution)/shard_map/psum | solution.py:93
  153.3 3.0 collective-permute-start.13
  154.3 4.4 %collective-permute-start.12 = (bf16[1,96,256]{2,1,0:T(8,128)(2,1)S(1)}, bf16[1,96,256]{2,1,0:T(8,128)(2,1)S(1)}, u32[]{:S(2)}, u32[]{:S(2)}) collective-permute-start(bf16[1,96,256]{2,1,0:T(8,128)(2,1)S(1)} %get-tuple-element.51), channel_id=1, source_target_pairs={{0,4},{4,8},{8,12},{12,16},{16,20},{20,24},{24,28},{28,0},{1,5},{5... | collective-permute-start | bytes 147464 | tf_op jit(solution)/shard_map/ppermute | solution.py:13
  158.7 5.2 %collective-permute-start.15 = (bf16[18,1,256]{2,1,0:T(2,128)(2,1)S(1)}, bf16[18,1,256]{2,1,0:T(2,128)(2,1)S(1)}, u32[]{:S(2)}, u32[]{:S(2)}) collective-permute-start(bf16[18,1,256]{2,1,0:T(2,128)(2,1)S(1)} %get-tuple-element.44), channel_id=1, source_target_pairs={{1,0},{2,1},{3,2},{0,3},{5,4},{6,5},{7,6},{4,7},{9,8},{10,9},{11,1... | collective-permute-start | bytes 27656 | tf_op jit(solution)/shard_map/ppermute | solution.py:16
  162.1 6.1 %collective-permute-start.14 = (bf16[18,1,256]{2,1,0:T(2,128)(2,1)S(1)}, bf16[18,1,256]{2,1,0:T(2,128)(2,1)S(1)}, u32[]{:S(2)}, u32[]{:S(2)}) collective-permute-start(bf16[18,1,256]{2,1,0:T(2,128)(2,1)S(1)} %get-tuple-element.43), channel_id=1, source_target_pairs={{0,1},{1,2},{2,3},{3,0},{4,5},{5,6},{6,7},{7,4},{8,9},{9,10},{10,1... | collective-permute-start | bytes 27656 | tf_op jit(solution)/shard_map/ppermute | solution.py:13
  327.9 3.4 copy-start.2
Sparse Core Ops, SparseCore 0:
  69.1 84.0 all-reduce.4
  155.7 172.1 all-reduce.6
